TPU v7x, 128 devices: a whole 4x4x4 slice. The times are simulated.
128 devices in a mesh: tp: 16 (over x_lo, z, core), seq: 8 (over y, x_hi).
Axes of the slice: x: 4 (x_hi: 2, x_lo: 2; x = x_hi * 2 + x_lo), y: 4, z: 4, core: 2. Of those that a mesh axis runs over, the one named last changes fastest.
Arguments:
- residual: bfloat16 [2048, 4096], P('seq'), may hold values from -6 to 6
- mix_gain: float32 [4096], replicated, may hold values from 0.5 to 1.5
- in_proj: bfloat16 [4096, 4096], P(None, 'tp'), may hold values from -0.09375 to 0.09375
- branch_proj: bfloat16 [4096, 4096], P(None, 'tp'), may hold values from -0.09375 to 0.09375
- conv_weight: float32 [4, 4096], P(None, 'tp'), may hold values from -3 to 3
- conv_bias: float32 [4096], P('tp'), may hold values from -1.25 to 1.25
- input_gate: bfloat16 [16, 256, 256], P('tp'), may hold values from -0.375 to 0.375
- input_bias: float32 [4096], P('tp'), may hold values from -3 to 3
- decay_gate: bfloat16 [16, 256, 256], P('tp'), may hold values from -0.375 to 0.375
- decay_bias: float32 [4096], P('tp'), may hold values from -3 to 3
- decay_param: float32 [4096], P('tp'), may hold values from -13 to -2, as said below
- out_proj: bfloat16 [4096, 4096], P('tp'), may hold values from -0.25 to 0.25
- mlp_gain: float32 [4096], replicated, may hold values from 0.5 to 1.5
- gate_proj: bfloat16 [4096, 12288], P('seq', 'tp'), may hold values from -0.09375 to 0.09375
- up_proj: bfloat16 [4096, 12288], P('seq', 'tp'), may hold values from -0.09375 to 0.09375
- down_proj: bfloat16 [12288, 4096], P('tp'), may hold values from -0.078125 to 0.078125
Outputs:
- updated: bfloat16 [2048, 4096], P('seq')
Inputs may be any that keep to these rules, and one draw needn't show every extreme that they name: softplus(decay_param) lies between 0.02 / 2048 and 0.1 for every channel.
All inputs are finite; a program needn't handle non-finite values.
Results may differ from a plain program's by a relative error of at most 0.02.
Values may be sent and summed in bfloat16 or wider, within the bound.
A program may use at most 128 MiB of HBM per device.

v0:
```python
import jax
import jax.numpy as jnp
from jax import lax
from jax.sharding import Mesh
from jax.sharding import PartitionSpec as P

SEQ = ("seq_0", "seq_1")
epsilon = 1e-06


def from_behind(value, axis, steps):
    count = lax.axis_size(axis)
    leading, last = (max(0, -steps), min(count, count - steps))
    return lax.ppermute(value, axis, [(source, source + steps) for source in range(leading, last)])


def whole_of(shard, axes, dim):
    for axis in reversed(axes):
        shard = lax.all_gather(shard, axis, axis=dim, tiled=True)
    return shard


def folded(shard, axis, dim, absorb, state):
    everything = jax.tree.map(lambda a: lax.all_gather(a, axis, axis=dim, tiled=True), shard)
    return absorb(state, everything, jnp.int32(0))


def rms_norm(values, gain):
    wide = values.astype(jnp.float32)
    factor = lax.rsqrt(jnp.mean(wide * wide, axis=-1, keepdims=True) + epsilon)
    return (wide * factor * gain).astype(jnp.bfloat16)


def block_gates(values, weight, bias):
    heads, width = (weight.shape[0], weight.shape[1])
    grouped = values.reshape(values.shape[0], heads, width)
    mixed = jnp.einsum("thi,hij->thj", grouped, weight, preferred_element_type=jnp.float32)
    return jax.nn.sigmoid(mixed.reshape(values.shape[0], heads * width) + bias)


def smooth(inner, tail, conv_weight, conv_bias):
    taps = conv_weight.shape[0]
    length = inner.shape[0]
    padded = jnp.concatenate([tail, inner], axis=0).astype(jnp.float32)
    total = conv_bias + jnp.zeros((length, inner.shape[1]), jnp.float32)
    for offset in range(taps):
        total = total + conv_weight[offset] * padded[taps - 1 - offset : taps - 1 - offset + length]
    return lax.optimization_barrier(total.astype(jnp.bfloat16))


def combine_state(earlier, later):
    return (earlier[0] * later[0], later[0] * earlier[1] + later[1])


def channel_total(partial_value):
    return lax.psum(partial_value.astype(jnp.bfloat16), "tp").astype(jnp.float32)


def on_device(
    residual,
    mix_gain,
    in_proj,
    branch_proj,
    conv_weight,
    conv_bias,
    input_gate,
    input_bias,
    decay_gate,
    decay_bias,
    decay_param,
    out_proj,
    mlp_gain,
    gate_proj,
    up_proj,
    down_proj,
):
    length = residual.shape[0]
    taps = conv_weight.shape[0]
    normed = rms_norm(residual, mix_gain)
    branch = jax.nn.gelu(
        jnp.dot(normed, branch_proj, preferred_element_type=jnp.float32), approximate=True
    )
    inner = jnp.dot(normed, in_proj, preferred_element_type=jnp.float32).astype(jnp.bfloat16)
    tail = from_behind(inner[length - (taps - 1) :], SEQ, 1)
    smoothed = smooth(inner, tail, conv_weight, conv_bias)
    input_rate = block_gates(smoothed, input_gate, input_bias)
    decay_rate = block_gates(smoothed, decay_gate, decay_bias)
    log_decay = -8.0 * decay_rate * jax.nn.softplus(decay_param)
    decay = jnp.exp(log_decay)
    position = lax.axis_index(SEQ)
    first = jnp.logical_and(position == 0, jnp.arange(length) == 0)[:, None]
    scale_in = jnp.where(first, 1.0, jnp.sqrt(-jnp.expm1(2.0 * log_decay)))
    pushed = smoothed.astype(jnp.float32) * input_rate * scale_in
    decays, partial_states = lax.associative_scan(combine_state, (decay, pushed), axis=0)
    end_decay = decays[-1]
    end_state = partial_states[-1]
    summaries = whole_of(jnp.stack([end_decay, end_state])[None], SEQ, 0)

    def fold(index, state):
        moved = summaries[index, 0] * state + summaries[index, 1]
        return jnp.where(index < position, moved, state)

    carried = lax.fori_loop(0, summaries.shape[0], fold, jnp.zeros_like(end_state))
    states = partial_states + decays * carried[None]
    gated = (states * branch).astype(jnp.bfloat16)
    mixed = channel_total(jnp.dot(gated, out_proj, preferred_element_type=jnp.float32))
    middle = lax.optimization_barrier((residual.astype(jnp.float32) + mixed).astype(jnp.bfloat16))
    hidden_in = rms_norm(middle, mlp_gain)
    width = gate_proj.shape[1]
    empty = jnp.zeros((length, width), jnp.float32)

    def add_rows(totals, pieces, start):
        columns = lax.dynamic_slice_in_dim(hidden_in, start, pieces[0].shape[0], 1)
        return (
            totals[0] + jnp.dot(columns, pieces[0], preferred_element_type=jnp.float32),
            totals[1] + jnp.dot(columns, pieces[1], preferred_element_type=jnp.float32),
        )

    gate, up = folded((gate_proj, up_proj), SEQ, 0, add_rows, (empty, empty))
    hidden = (jax.nn.gelu(gate, approximate=True) * up).astype(jnp.bfloat16)
    output = channel_total(jnp.dot(hidden, down_proj, preferred_element_type=jnp.float32))
    return (middle.astype(jnp.float32) + output).astype(jnp.bfloat16)


def solution(mesh):
    split = Mesh(mesh.devices.reshape(mesh.shape["tp"], 4, 2), ("tp", "seq_0", "seq_1"))
    in_specs = (
        P(SEQ, None),
        P(),
        P(None, "tp"),
        P(None, "tp"),
        P(None, "tp"),
        P("tp"),
        P("tp", None, None),
        P("tp"),
        P("tp", None, None),
        P("tp"),
        P("tp"),
        P("tp", None),
        P(),
        P(SEQ, "tp"),
        P(SEQ, "tp"),
        P("tp", None),
    )
    out_specs = P(SEQ, None)
    return jax.shard_map(
        on_device, mesh=split, in_specs=in_specs, out_specs=out_specs, check_vma=False
    )
```

profile of v0, /device:TPU:1, one launch (start us, length us, event | category | flops | bytes accessed | tf_op | source)
XLA Modules:
  0.0 404.2 jit_solution(9161906247059077176)
XLA Ops:
  7.4 2.2 fusion
  9.8 2.5 convolution_convert_fusion.2
  12.3 5.6 %collective-permute-start = (bf16[3,256]{1,0:T(4,128)(2,1)S(1)}, bf16[3,256]{1,0:T(4,128)(2,1)S(1)}, u32[]{:S(2)}, u32[]{:S(2)}) collective-permute-start(bf16[3,256]{1,0:T(4,128)(2,1)S(1)} %slice.348), channel_id=1, source_target_pairs={{0,1},{1,2},{2,3},{3,4},{4,5},{5,6},{6,7},{8,9},{9,10},{10,11},{11... | collective-permute-start | bytes 4616 | tf_op jit(solution)/shard_map/ppermute | solution.py:14
  18.0 0.6 collective-permute-done
  18.8 0.3 fusion.93
  19.1 0.3 fusion.19
  20.9 0.2 slice.330
  21.2 0.2 slice.273
  22.5 0.3 slice-done
  22.9 4.9 %all-gather.1 = f32[2,2,256]{2,1,0:T(2,128)S(1)} all-gather(f32[1,2,256]{2,1,0:T(2,128)S(1)} %maximum_bitcast_fusion), channel_id=2, replica_groups=mesh['tp'=16,'seq_0'=4,'seq_1'=2] {'seq_1'}, dimensions={0}, use_global_device_ids=true | all-gather | bytes 6144 | tf_op jit(solution)/shard_map/all_gather | solution.py:19
  27.9 10.8 %all_gather.13 = f32[8,2,256]{2,1,0:T(2,128)S(1)} all-gather(f32[2,2,256]{2,1,0:T(2,128)S(1)} %all-gather.1), channel_id=1, replica_groups=mesh['tp'=16,'seq_0'=4,'seq_1'=2] {'seq_0'}, dimensions={0}, use_global_device_ids=true | all-gather | bytes 20480 | tf_op jit(solution)/shard_map/all_gather | solution.py:19
  38.6 0.4 while.14
  39.1 6.0 %convolution_convert_fusion = bf16[256,4096]{1,0:T(8,128)(2,1)} fusion(bf16[256,4096]{1,0:T(8,128)(2,1)S(1)} %copy-done, bf16[4096,256]{1,0:T(8,128)(2,1)} %param.21, bf16[256,4096]{1,0:T(8,128)(2,1)} %param.18, f32[4096]{0:T(1024)} %param.19, f32[256]{0:T(256)S(1)} %add_rsqrt_fusion.1, f32[256,256]{1,0:T(8,128)S(1)} %pad.128, f32[256,256]{1,0:T(8,128)S(1)} %pad.129, ...), kind=kOutput, calls=%fused_computation.9 | convolution fusion | flops 1079902208 | bytes 9455616 | tf_op jit(solution)/shard_map/dot_general | solution.py:106
  45.2 0.5 all-gather.5.cloned.1.call-update
  45.7 0.5 all-gather.7.cloned.1.call-update
  46.3 0.2 all-reduce.37.cloned.1.call-start
  46.5 198.7 %all-reduce.35.cloned.1.call-done = bf16[256,4096]{1,0:T(8,128)(2,1)} async-done(((bf16[256,4096]{1,0:T(8,128)(2,1)}), bf16[256,4096]{1,0:T(8,128)(2,1)}) %all-reduce.35.cloned.1.call-update) | async-done | bytes 2097168 | tf_op jit(solution)/shard_map/psum | solution.py:56
  245.2 3.0 fusion.3
  248.2 1.3 copy-done.1
  249.5 0.5 fusion.4
  250.2 5.3 %fusion.29 = f32[256,768]{1,0:T(8,128)S(1)} fusion(bf16[4096,768]{1,0:T(8,128)(2,1)} %all-gather.5.cloned.1.call-done, bf16[256,4096]{1,0:T(8,128)(2,1)} %copy-done.1, f32[4096]{0:T(1024)S(1)} %copy-done.9, f32[256]{0:T(256)S(1)} %add_rsqrt_fusion), kind=kOutput, calls=%fused_computation.43 | convolution fusion | flops 1614807040 | bytes 9192448 | tf_op jit(solution)/shard_map/dot_general | solution.py:115
  255.5 11.3 %convolution_convert_fusion.1 = bf16[256,4096]{1,0:T(8,128)(2,1)} fusion(bf16[768,4096]{1,0:T(8,128)(2,1)} %param.33, bf16[4096,768]{1,0:T(8,128)(2,1)} %all-gather.7.cloned.1.call-done, f32[256,768]{1,0:T(8,128)S(1)} %fusion.29, bf16[256,4096]{1,0:T(8,128)(2,1)} %copy-done.1, f32[4096]{0:T(1024)S(1)} %copy-done.9, f32[256]{0:T(256)S(1)} %add_rsqrt_fusion), kind=kOutput, calls=%fused_computation.10 | convolution fusion | flops 3228434432 | bytes 17581056 | tf_op jit(solution)/shard_map/dot_general | solution.py:121
  266.8 125.6 %all-reduce.37.cloned.1.call-done = bf16[256,4096]{1,0:T(8,128)(2,1)} async-done(((bf16[256,4096]{1,0:T(8,128)(2,1)}), bf16[256,4096]{1,0:T(8,128)(2,1)}) %all-reduce.37.cloned.1.call-update) | async-done | bytes 2097168 | tf_op jit(solution)/shard_map/psum | solution.py:56
  392.4 4.3 %fusion.7 = bf16[256,4096]{1,0:T(8,128)(2,1)} fusion(bf16[256,4096]{1,0:T(8,128)(2,1)} %copy-done.1, bf16[256,4096]{1,0:T(8,128)(2,1)} %all-reduce.37.cloned.1.call-done), kind=kLoop, calls=%fused_computation.18 | loop fusion | flops 4194304 | bytes 6291456 | tf_op jit(solution)/shard_map/convert_element_type | solution.py:122
  (177 shorter events, 3.0 us)
Async XLA Ops:
  7.4 31.7 %copy-start = (bf16[256,4096]{1,0:T(8,128)(2,1)S(1)}, bf16[256,4096]{1,0:T(8,128)(2,1)}, u32[]{:S(2)}) copy-start(bf16[256,4096]{1,0:T(8,128)(2,1)} %param.29) | copy-start | bytes 6291460
  7.4 237.8 %all-reduce.35.cloned.1.call-start = ((), (), s32[]{:S(2)}) async-start(), calls=%async_computation | async-start | bytes 4194304 | tf_op jit(solution)/shard_map/psum | solution.py:56
  7.4 2.4 copy-start.2
  9.7 8.2 %copy-start.4 = (f32[4,256]{1,0:T(4,128)S(1)}, f32[4,256]{1,0:T(4,128)}, u32[]{:S(2)}) copy-start(f32[4,256]{1,0:T(4,128)} %param.22) | copy-start | bytes 12292
  9.7 8.2 %copy-start.5 = (f32[256]{0:T(256)S(1)}, f32[256]{0:T(256)}, u32[]{:S(2)}) copy-start(f32[256]{0:T(256)} %param.28) | copy-start | bytes 3076
  9.7 8.9 %copy-start.6 = (f32[256]{0:T(256)S(1)}, f32[256]{0:T(256)}, u32[]{:S(2)}) copy-start(f32[256]{0:T(256)} %param.23) | copy-start | bytes 3076
  9.8 9.0 %copy-start.7 = (bf16[1,256,256]{2,1,0:T(8,128)(2,1)S(1)}, bf16[1,256,256]{2,1,0:T(8,128)(2,1)}, u32[]{:S(2)}) copy-start(bf16[1,256,256]{2,1,0:T(8,128)(2,1)} %param.26) | copy-start | bytes 393220
  9.8 9.1 %copy-start.10 = (f32[256]{0:T(256)S(1)}, f32[256]{0:T(256)}, u32[]{:S(2)}) copy-start(f32[256]{0:T(256)} %param.27) | copy-start | bytes 3076
  12.2 6.8 %copy-start.8 = (bf16[1,256,256]{2,1,0:T(8,128)(2,1)S(1)}, bf16[1,256,256]{2,1,0:T(8,128)(2,1)}, u32[]{:S(2)}) copy-start(bf16[1,256,256]{2,1,0:T(8,128)(2,1)} %param.24) | copy-start | bytes 393220
  12.3 6.8 %copy-start.11 = (f32[256]{0:T(256)S(1)}, f32[256]{0:T(256)}, u32[]{:S(2)}) copy-start(f32[256]{0:T(256)} %param.25) | copy-start | bytes 3076
  12.3 6.3 %collective-permute-start = (bf16[3,256]{1,0:T(4,128)(2,1)S(1)}, bf16[3,256]{1,0:T(4,128)(2,1)S(1)}, u32[]{:S(2)}, u32[]{:S(2)}) collective-permute-start(bf16[3,256]{1,0:T(4,128)(2,1)S(1)} %slice.348), channel_id=1, source_target_pairs={{0,1},{1,2},{2,3},{3,4},{4,5},{5,6},{6,7},{8,9},{9,10},{10,11},{11... | collective-permute-start | bytes 4616 | tf_op jit(solution)/shard_map/ppermute | solution.py:14
  19.4 2.0 copy-start.3
  22.1 0.7 slice-start
  45.1 204.9 %all-gather.5.cloned.1.call-start = ((), (), s32[]{:S(2)}) async-start(), calls=%async_computation.1 | async-start | bytes 7077888 | tf_op jit(solution)/shard_map/all_gather | solution.py:24
  45.7 209.8 %all-gather.7.cloned.1.call-start = ((), (), s32[]{:S(2)}) async-start(), calls=%async_computation.2 | async-start | bytes 7077888 | tf_op jit(solution)/shard_map/all_gather | solution.py:24
  46.3 346.1 %all-reduce.37.cloned.1.call-start = ((), (), s32[]{:S(2)}) async-start(), calls=%async_computation.3 | async-start | bytes 4194304 | tf_op jit(solution)/shard_map/psum | solution.py:56
  248.2 1.3 copy-start.1
  249.5 0.7 copy-start.9
Sparse Core Ops, SparseCore 0:
  45.2 199.8 all-reduce.34
  266.9 125.4 all-reduce.36
Sparse Core Ops, SparseCore 1:
  47.9 93.9 all-gather.4
  144.0 85.9 all-gather.6
where the time goes:
time: 404 us
  waiting for transfers between devices  326 us (81%)
  matrix products  25.6 us (6%)
  between operations  15.8 us (4%)
  blocking collectives  15.7 us (4%)
  other arithmetic  10.9 us (3%)
  starting transfers between devices  5.91 us (1%)
  local copies, waits for them, and re-layouts  4.04 us (1%)
    psum x2, waiting for transfers between devices, channel_total(): lax.psum(partial_value.astype(jnp.bfloat16), 'tp').astype(jnp.float32)  324 us
    all_gather x2, blocking collectives, whole_of(): shard = lax.all_gather(shard, axis, axis=dim, tiled=True)  15.7 us
    dot_general x1, matrix products, on_device(): jnp.dot(hidden, down_proj, preferred_element_type=jnp.float32)  11.3 us
  transfers between devices with their start and end apart: 5, of which 3 were waited for; matrix products, arithmetic and copies ran while one was open for 2% of the time, Pallas kernels for 0%

commit v1 on v0

--- a/solution.py
+++ b/solution.py
@@ -53,7 +53,9 @@
 
 
 def channel_total(partial_value):
-    return lax.psum(partial_value.astype(jnp.bfloat16), "tp").astype(jnp.float32)
+    return jnp.sum(lax.all_gather(partial_value.astype(jnp.bfloat16), "tp"), axis=0).astype(
+        jnp.float32
+    )
 
 
 def on_device(

time: 404 us -> 605 us (1.50)
  waiting for transfers between devices: 326 us -> 505 us
  other arithmetic: 10.9 us -> 37.3 us
    all_gather x0 -> x2, waiting for transfers between devices: none -> 345 us  [channel_total(): lax.all_gather(partial_value.astype(jnp.bfloat16), 'tp')]
    psum x2 -> x0, waiting for transfers between devices: 324 us -> none  [channel_total(): lax.psum(partial_value.astype(jnp.bfloat16), 'tp').astype(jnp.float32)]
    all_gather x2, waiting for transfers between devices: 0.05 us -> 158 us  [folded(): lax.all_gather(a, axis, axis=dim, tiled=True)]
    reduce_sum x0 -> x2, other arithmetic: none -> 26.1 us  [channel_total(): jnp.sum(lax.all_gather(partial_value.astype(jnp.bfloat16), 'tp'), axis=0)]
  transfers between devices with their start and end apart: 5 -> 5, of which waited for: 3 -> 5; matrix products, arithmetic and copies ran while one was open for 2% -> 4% of each run, Pallas kernels for 0% -> 0%
where the time goes in v1:
time: 605 us
  waiting for transfers between devices  505 us (83%)
  other arithmetic  37.3 us (6%)
  matrix products  24.3 us (4%)
  blocking collectives  15.7 us (3%)
  between operations  14 us (2%)
    all_gather x2, waiting for transfers between devices, channel_total(): lax.all_gather(partial_value.astype(jnp.bfloat16), 'tp')  345 us
    all_gather x2, waiting for transfers between devices, folded(): lax.all_gather(a, axis, axis=dim, tiled=True)  158 us
    reduce_sum x2, other arithmetic, channel_total(): jnp.sum(lax.all_gather(partial_value.astype(jnp.bfloat16), 'tp'), axis=0)  26.1 us
    all_gather x2, blocking collectives, whole_of(): shard = lax.all_gather(shard, axis, axis=dim, tiled=True)  15.7 us
  transfers between devices with their start and end apart: 5, of which 5 were waited for; matrix products, arithmetic and copies ran while one was open for 4% of the time, Pallas kernels for 0%

profile of v1, /device:TPU:1, one launch (start us, length us, event | category | flops | bytes accessed | tf_op | source)
XLA Modules:
  0.0 605.2 jit_solution(12152965135691595950)
XLA Ops:
  6.5 2.2 fusion
  8.9 2.5 convolution_convert_fusion.2
  11.4 5.6 collective-permute-start
  17.2 0.6 collective-permute-done
  18.0 0.3 fusion.93
  18.3 0.3 fusion.19
  21.7 0.3 slice-done
  22.1 4.9 all-gather.3
  27.0 10.8 %all_gather.25 = f32[8,2,256]{2,1,0:T(2,128)S(1)} all-gather(f32[2,2,256]{2,1,0:T(2,128)S(1)} %all-gather.3), channel_id=1, replica_groups=mesh['tp'=16,'seq_0'=4,'seq_1'=2] {'seq_0'}, dimensions={0}, use_global_device_ids=true | all-gather | bytes 20480 | tf_op jit(solution)/shard_map/all_gather | solution.py:19
  37.8 0.4 while.14
  38.2 6.0 convolution_convert_fusion
  44.3 0.7 all-gather.9.cloned.1.call-update
  45.1 0.7 all-gather.11.cloned.1.call-update
  46.0 175.4 %all-gather.13.cloned.1.call-done = bf16[4096,4096]{1,0:T(8,128)(2,1)} async-done(((bf16[256,4096]{1,0:T(8,128)(2,1)}), bf16[4096,4096]{1,0:T(8,128)(2,1)}) %all-gather.13.cloned.1.call-update) | async-done | bytes 33554448 | tf_op jit(solution)/shard_map/all_gather | solution.py:56
  221.4 13.0 %reduce_sum.43 = bf16[256,4096]{1,0:T(8,128)(2,1)} reduce(bf16[16,256,4096]{2,1,0:T(8,128)(2,1)} %bitcast.30, bf16[]{:T(256)} %constant.65.clone.1), dimensions={0}, to_apply=%region_3.4 | reduce | flops 15728640 | bytes 35651584 | tf_op jit(solution)/shard_map/reduce_sum | solution.py:56
  234.4 3.4 fusion.3
  237.8 0.5 fusion.4
  238.3 73.8 %all-gather.9.cloned.1.call-done = bf16[4096,768]{1,0:T(8,128)(2,1)} async-done(((bf16[512,768]{1,0:T(8,128)(2,1)}), bf16[4096,768]{1,0:T(8,128)(2,1)}) %all-gather.9.cloned.1.call-update) | async-done | bytes 6291472 | tf_op jit(solution)/shard_map/all_gather | solution.py:24
  312.1 4.6 fusion.29
  316.7 84.1 %all-gather.11.cloned.1.call-done = bf16[4096,768]{1,0:T(8,128)(2,1)} async-done(((bf16[512,768]{1,0:T(8,128)(2,1)}), bf16[4096,768]{1,0:T(8,128)(2,1)}) %all-gather.11.cloned.1.call-update) | async-done | bytes 6291472 | tf_op jit(solution)/shard_map/all_gather | solution.py:24
  400.8 10.6 %convolution_convert_fusion.1 = bf16[256,4096]{1,0:T(8,128)(2,1)} fusion(bf16[768,4096]{1,0:T(8,128)(2,1)} %param.33, bf16[4096,768]{1,0:T(8,128)(2,1)} %all-gather.11.cloned.1.call-done, f32[256,768]{1,0:T(8,128)S(1)} %fusion.29, bf16[256,4096]{1,0:T(8,128)(2,1)S(1)} %fusion.3, f32[4096]{0:T(1024)S(1)} %copy-done.10, f32[256]{0:T(256)S(1)} %add_rsqrt_fusion), kind=kOutput, calls=%fused_computation.10 | convolution fusion | flops 3228434432 | bytes 17581056 | tf_op jit(solution)/shard_map/dot_general | solution.py:123
  411.4 169.8 %all-gather.15.cloned.1.call-done = bf16[4096,4096]{1,0:T(8,128)(2,1)} async-done(((bf16[256,4096]{1,0:T(8,128)(2,1)}), bf16[4096,4096]{1,0:T(8,128)(2,1)}) %all-gather.15.cloned.1.call-update) | async-done | bytes 33554448 | tf_op jit(solution)/shard_map/all_gather | solution.py:56
  581.2 13.1 %reduce_sum.45 = bf16[256,4096]{1,0:T(8,128)(2,1)} reduce(bf16[16,256,4096]{2,1,0:T(8,128)(2,1)} %bitcast.31, bf16[]{:T(256)} %constant.65.clone.1), dimensions={0}, to_apply=%region_5.6 | reduce | flops 15728640 | bytes 35651584 | tf_op jit(solution)/shard_map/reduce_sum | solution.py:56
  594.3 4.3 fusion.7
  (181 shorter events, 3.4 us)
Async XLA Ops:
  6.5 31.7 %copy-start = (bf16[256,4096]{1,0:T(8,128)(2,1)S(1)}, bf16[256,4096]{1,0:T(8,128)(2,1)}, u32[]{:S(2)}) copy-start(bf16[256,4096]{1,0:T(8,128)(2,1)} %param.29) | copy-start | bytes 6291460
  6.5 214.9 %all-gather.13.cloned.1.call-start = ((), (), s32[]{:S(2)}) async-start(), calls=%async_computation.2 | async-start | bytes 35651584 | tf_op jit(solution)/shard_map/all_gather | solution.py:56
  6.5 2.4 copy-start.3
  8.9 8.2 %copy-start.5 = (f32[4,256]{1,0:T(4,128)S(1)}, f32[4,256]{1,0:T(4,128)}, u32[]{:S(2)}) copy-start(f32[4,256]{1,0:T(4,128)} %param.22) | copy-start | bytes 12292
  8.9 8.2 %copy-start.6 = (f32[256]{0:T(256)S(1)}, f32[256]{0:T(256)}, u32[]{:S(2)}) copy-start(f32[256]{0:T(256)} %param.28) | copy-start | bytes 3076
  8.9 8.9 %copy-start.7 = (f32[256]{0:T(256)S(1)}, f32[256]{0:T(256)}, u32[]{:S(2)}) copy-start(f32[256]{0:T(256)} %param.23) | copy-start | bytes 3076
  8.9 9.1 %copy-start.8 = (bf16[1,256,256]{2,1,0:T(8,128)(2,1)S(1)}, bf16[1,256,256]{2,1,0:T(8,128)(2,1)}, u32[]{:S(2)}) copy-start(bf16[1,256,256]{2,1,0:T(8,128)(2,1)} %param.26) | copy-start | bytes 393220
  8.9 9.1 %copy-start.11 = (f32[256]{0:T(256)S(1)}, f32[256]{0:T(256)}, u32[]{:S(2)}) copy-start(f32[256]{0:T(256)} %param.27) | copy-start | bytes 3076
  11.4 6.9 %copy-start.9 = (bf16[1,256,256]{2,1,0:T(8,128)(2,1)S(1)}, bf16[1,256,256]{2,1,0:T(8,128)(2,1)}, u32[]{:S(2)}) copy-start(bf16[1,256,256]{2,1,0:T(8,128)(2,1)} %param.24) | copy-start | bytes 393220
  11.4 6.9 %copy-start.12 = (f32[256]{0:T(256)S(1)}, f32[256]{0:T(256)}, u32[]{:S(2)}) copy-start(f32[256]{0:T(256)} %param.25) | copy-start | bytes 3076
  11.4 6.3 %collective-permute-start = (bf16[3,256]{1,0:T(4,128)(2,1)S(1)}, bf16[3,256]{1,0:T(4,128)(2,1)S(1)}, u32[]{:S(2)}, u32[]{:S(2)}) collective-permute-start(bf16[3,256]{1,0:T(4,128)(2,1)S(1)} %slice.348), channel_id=1, source_target_pairs={{0,1},{1,2},{2,3},{3,4},{4,5},{5,6},{6,7},{8,9},{9,10},{10,11},{11... | collective-permute-start | bytes 4616 | tf_op jit(solution)/shard_map/ppermute | solution.py:14
  18.6 2.0 copy-start.4
  21.3 0.7 slice-start
  44.3 267.8 %all-gather.9.cloned.1.call-start = ((), (), s32[]{:S(2)}) async-start(), calls=%async_computation | async-start | bytes 7077888 | tf_op jit(solution)/shard_map/all_gather | solution.py:24
  45.0 355.8 %all-gather.11.cloned.1.call-start = ((), (), s32[]{:S(2)}) async-start(), calls=%async_computation.1 | async-start | bytes 7077888 | tf_op jit(solution)/shard_map/all_gather | solution.py:24
  45.8 535.5 %all-gather.15.cloned.1.call-start = ((), (), s32[]{:S(2)}) async-start(), calls=%async_computation.3 | async-start | bytes 35651584 | tf_op jit(solution)/shard_map/all_gather | solution.py:56
  237.8 163.0 %copy-start.2 = (bf16[256,4096]{1,0:T(8,128)(2,1)}, bf16[256,4096]{1,0:T(8,128)(2,1)S(1)}, u32[]{:S(2)}) copy-start(bf16[256,4096]{1,0:T(8,128)(2,1)S(1)} %fusion.3) | copy-start | bytes 6291460
  237.8 74.3 %copy-start.10 = (f32[4096]{0:T(1024)S(1)}, f32[4096]{0:T(1024)}, u32[]{:S(2)}) copy-start(f32[4096]{0:T(1024)} %param.30) | copy-start | bytes 49156
  581.2 17.4 %copy-start.1 = (bf16[256,4096]{1,0:T(8,128)(2,1)S(1)}, bf16[256,4096]{1,0:T(8,128)(2,1)}, u32[]{:S(2)}) copy-start(bf16[256,4096]{1,0:T(8,128)(2,1)} %param.29) | copy-start | bytes 6291460
Sparse Core Ops, SparseCore 0:
  44.4 176.9 all-gather.12
  223.7 88.2 all-gather.8
  314.4 86.3 all-gather.10
  411.5 169.6 all-gather.14
